TPU v7x, 32 devices: a whole 2x2x4 slice. The times are simulated.
32 devices in a mesh: stream: 8 (over y, x, core), leaf: 4 (over z).
Axes of the slice: x: 2, y: 2, z: 4, core: 2. Of those that a mesh axis runs over, the one named last changes fastest.
Arguments:
- points_rhs: bfloat16 [2048, 32, 128], P(('stream', 'leaf')), may hold values from -6 to 6
- leaf_basis: bfloat16 [2048, 64, 128], P(('stream', 'leaf')), may hold values from -0.5 to 0.5
- transfer: bfloat16 [1024, 64, 128], P(('stream', 'leaf')), may hold values from -0.5 to 0.5
- leaf_coupling: bfloat16 [2048, 64, 256], P(('stream', 'leaf')), may hold values from -0.375 to 0.375
- parent_coupling: bfloat16 [1024, 64, 512], P(('stream', 'leaf')), may hold values from -0.25 to 0.25
- near_blocks: bfloat16 [2048, 3, 128, 128], P(('stream', 'leaf')), may hold values from -0.3125 to 0.3125
- near_offsets: int32 [2048, 3], P(('stream', 'leaf')), may hold values from -2 to 2, as said below
- coupling_offsets: int32 [2048, 4], P(('stream', 'leaf')), may hold values from -5 to 5, as said below
- parent_owner: int32 [1024, 8], P(('stream', 'leaf')), may hold values from 0 to 31, all different within a row; in each aligned block of 32 rows (0 to 31, 32 to 63, ...) at most 16 rows name the same one
- parent_local: int32 [1024, 8], P(('stream', 'leaf')), may hold values from 0 to 31
Outputs:
- product: bfloat16 [2048, 32, 128], P(('stream', 'leaf'))
Inputs may be any that keep to these rules, and one draw needn't show every extreme that they name: `near_offsets`: each row holds 3 different offsets; the first is 0. `coupling_offsets`: each row holds 4 different nonzero offsets, none of which stands in the same row of near_offsets. `parent_owner`: each row names 8 different blocks; the rows of one device name no block more than 16 times, and in every draw some block is named exactly 16 times by the rows of some device.
All inputs are finite; a program needn't handle non-finite values.
Results may differ from a plain program's by a relative error of at most 0.0053.
Values may be sent and summed in bfloat16 or wider, within the bound.
A program may use at most 128 MiB of HBM per device.

v0:
```python
import functools

import jax
import jax.numpy as jnp
from jax import lax
from jax.experimental import pallas as pl
from jax.experimental.pallas import tpu as pltpu
from jax.sharding import PartitionSpec as P

NEAR_REACH = 2
FAR_REACH = 5
MESH = pl.DeviceIdType.MESH
NT = (((1,), (1,)), ((), ()))
NN = (((1,), (0,)), ((), ()))


def dot(a, b, dims):
    return lax.dot_general(a, b, dims, preferred_element_type=jnp.float32)


def bits_of(count):
    bits = count.bit_length() - 1
    assert 1 << bits == count
    return bits


def kernel(
    streams, line,
    near_off, far_off, owner, local,
    points_hbm, basis_hbm, transfer_hbm, leaf_hbm, parent_hbm, near_hbm,
    out_hbm,
    points, basis, transfer, leaf_panel, parent_panel, near_blocks,
    coeffs, gathered, near_sum, leaf_sum, out,
    load_sem, near_sem, out_sem, halo_send, halo_recv, send_sem, recv_sem,
):
    leaves, rhs, size = points_hbm.shape
    parents, rank, _ = transfer_hbm.shape
    kn = near_off.shape[0]
    kc = far_off.shape[0]
    kp = owner.shape[0]
    half = rhs // 2
    width = 8
    parts = recv_sem.shape[0] // (streams * line)
    chunk = parents // parts
    nbits = bits_of(streams // 2)
    near_parts = near_sem.shape[0]
    out_parts = out_sem.shape[0]

    my_s = lax.axis_index("stream")
    my_z = lax.axis_index("leaf")
    core = my_s % 2
    place = my_s // 2
    total_blocks = streams * line
    me = my_s * line + my_z

    def device(block):
        return (block // line, block % line)

    def block_of(h, z):
        return (h * 2 + core) * line + z

    def bit_at(phase):
        first = 1 << phase
        if nbits < 2:
            return first
        second = 1 << ((phase + 1) % nbits)
        return first + core * (second - first)

    def flip(h, bit):
        return h + bit * (1 - 2 * ((h // bit) % 2))

    def subset(mask):
        h = place
        for phase in range(nbits):
            if mask >> phase & 1:
                h = flip(h, bit_at(phase))
        return h

    partners = [(flip(place, bit_at(i)) * 2 + core, my_z) for i in range(nbits)]
    line_peers = [(my_s, (my_z + t) % line) for t in range(1, line)]
    sibling = (my_s + 1 - 2 * core, my_z)
    after = device((me + 1) % total_blocks)
    before = device((me + total_blocks - 1) % total_blocks)

    loads = [
        pltpu.make_async_copy(points_hbm, points.at[pl.ds(NEAR_REACH, leaves)], load_sem.at[0]),
        pltpu.make_async_copy(basis_hbm, basis, load_sem.at[1]),
        pltpu.make_async_copy(transfer_hbm, transfer, load_sem.at[2]),
        pltpu.make_async_copy(leaf_hbm, leaf_panel, load_sem.at[3]),
        pltpu.make_async_copy(parent_hbm, parent_panel, load_sem.at[4]),
    ]
    near_rows = leaves // near_parts
    near_loads = [
        pltpu.make_async_copy(
            near_hbm.at[pl.ds(i * near_rows, near_rows)],
            near_blocks.at[pl.ds(i * near_rows, near_rows)],
            near_sem.at[i],
        )
        for i in range(near_parts)
    ]
    for load in loads[:3]:
        load.start()

    barrier = pltpu.get_barrier_semaphore()
    greeted = partners + line_peers + [sibling, after, before]
    for other in greeted:
        pl.semaphore_signal(barrier, inc=1, device_id=other, device_id_type=MESH)
    for load in near_loads + loads[3:]:
        load.start()

    low_lanes = lax.broadcasted_iota(jnp.int32, (rhs, 2 * rank), 1) < rank

    def upward(group, _):
        ps = [group * width + i for i in range(width)]
        boths = []
        for p in ps:
            pair = jnp.concatenate([points[NEAR_REACH + 2 * p], points[NEAR_REACH + 2 * p + 1]], axis=0)
            weights = basis[pl.ds(2 * p, 2)].reshape(2 * rank, size)
            boths.append(dot(pair, weights, NT))
        sides = [jnp.where(low_lanes, both[:rhs], both[rhs:]) for both in boths]
        ups = [dot(side.astype(jnp.bfloat16), transfer[p], NT) for p, side in zip(ps, sides)]
        for p, up in zip(ps, ups):
            packed = jnp.concatenate([up[:half], up[half:]], axis=1)
            gathered[me * parents + p] = packed.astype(jnp.bfloat16)
        for p, side in zip(ps, sides):
            turned = pltpu.roll(side, rank, 1)
            coeffs[FAR_REACH + 2 * p] = jnp.where(low_lanes, side, turned).astype(jnp.bfloat16)
            coeffs[FAR_REACH + 2 * p + 1] = jnp.where(low_lanes, turned, side).astype(jnp.bfloat16)
        return 0

    for load in loads[:3]:
        load.wait()
    groups = parents // width
    lax.fori_loop(0, 1, upward, 0)
    pl.semaphore_wait(barrier, len(greeted))

    def halo(index, source, target, whom):
        return pltpu.make_async_remote_copy(
            src_ref=source, dst_ref=target,
            send_sem=halo_send.at[index], recv_sem=halo_recv.at[index],
            device_id=whom, device_id_type=MESH,
        )

    point_halos = [
        halo(0, points_hbm.at[pl.ds(leaves - NEAR_REACH, NEAR_REACH)],
             points.at[pl.ds(0, NEAR_REACH)], after),
        halo(1, points_hbm.at[pl.ds(0, NEAR_REACH)],
             points.at[pl.ds(NEAR_REACH + leaves, NEAR_REACH)], before),
    ]
    for copy in point_halos:
        copy.start()

    coeff_halos = [
        halo(2, coeffs.at[pl.ds(leaves, FAR_REACH)], coeffs.at[pl.ds(0, FAR_REACH)], after),
        halo(3, coeffs.at[pl.ds(FAR_REACH, FAR_REACH)],
             coeffs.at[pl.ds(FAR_REACH + leaves, FAR_REACH)], before),
    ]

    sends = []

    def span(block, part):
        return gathered.at[pl.ds(block * parents + part * chunk, chunk)]

    def send(block, part, whom):
        copy = pltpu.make_async_remote_copy(
            src_ref=span(block, part), dst_ref=span(block, part),
            send_sem=send_sem.at[len(sends)], recv_sem=recv_sem.at[block * parts + part],
            device_id=whom, device_id_type=MESH,
        )
        copy.start()
        sends.append(copy)

    def arrived(block, part):
        pltpu.make_async_remote_copy(
            src_ref=span(block, part), dst_ref=span(block, part),
            send_sem=send_sem.at[0], recv_sem=recv_sem.at[block * parts + part],
            device_id=sibling, device_id_type=MESH,
        ).wait_recv()

    def send_own(part):
        for whom in line_peers[:2]:
            send(me, part, whom)
        for whom in reversed(partners):
            send(me, part, whom)
        for whom in line_peers[2:] + [sibling]:
            send(me, part, whom)

    per_part = groups // parts
    for part in range(parts):
        lax.fori_loop(max(1, part * per_part), (part + 1) * per_part, upward, 0)
        send_own(part)
    for copy in coeff_halos:
        copy.start()

    def relay(mask, t, part):
        def go():
            block = block_of(subset(mask), (my_z + t) % line)
            arrived(block, part)
            for phase in reversed(range(mask.bit_length(), nbits)):
                send(block, part, partners[phase])
            send(block, part, sibling)
        return go

    reach = [0] + [s for i in range(1, line) for s in (i, line - i)]
    order = list(dict.fromkeys(reach))

    def lag(mask):
        if mask == 0:
            return 0
        return 2 * line if mask == (1 << nbits) - 1 else bin(mask).count('1')

    events = [(parts * step + part + 3 * lag(mask), mask, part, order[step])
              for step in range(line) for mask in range(1 << nbits) for part in range(parts)
              if mask or order[step]]
    turns = [relay(mask, t, part) for _, mask, part, t in sorted(events)]

    pieces = 16
    done = [0]

    def advance(piece):
        upto = len(turns) * (piece + 1) // pieces
        for turn in turns[done[0]:upto]:
            turn()
        done[0] = upto

    first = me == 0
    last = me == total_blocks - 1

    for copy in point_halos:
        copy.wait()

    @pl.when(first)
    def _():
        points[pl.ds(0, NEAR_REACH)] = jnp.zeros((NEAR_REACH, rhs, size), jnp.bfloat16)

    @pl.when(last)
    def _():
        points[pl.ds(NEAR_REACH + leaves, NEAR_REACH)] = jnp.zeros(
            (NEAR_REACH, rhs, size), jnp.bfloat16)

    def near(group, _):
        cs = [group * width + i for i in range(width)]
        sums = []
        for c in cs:
            rows = [points[NEAR_REACH + c + near_off[k, c]] for k in range(kn)]
            weights = [near_blocks[c, k] for k in range(kn)]
            sums.append(dot(jnp.concatenate(rows, axis=1), jnp.concatenate(weights, axis=1), NT))
        for c, value in zip(cs, sums):
            near_sum[c] = value
        return 0

    per_piece = leaves // (pieces // 2)
    for piece in range(pieces // 2):
        for part in range(near_parts):
            if part * near_rows // per_piece == piece:
                near_loads[part].wait()
        lax.fori_loop(piece * per_piece // width, (piece + 1) * per_piece // width, near, 0)
        advance(piece)

    for copy in coeff_halos:
        copy.wait()

    @pl.when(first)
    def _():
        coeffs[pl.ds(0, FAR_REACH)] = jnp.zeros((FAR_REACH, rhs, 2 * rank), jnp.bfloat16)

    @pl.when(last)
    def _():
        coeffs[pl.ds(FAR_REACH + leaves, FAR_REACH)] = jnp.zeros(
            (FAR_REACH, rhs, 2 * rank), jnp.bfloat16)

    loads[3].wait()

    def one_leaf(c):
        rows = [coeffs[FAR_REACH + c + far_off[k, c]] for k in range(kc)]
        sides = [jnp.where(low_lanes, rows[k], rows[k + 1]) for k in range(0, kc, 2)]
        return dot(jnp.concatenate(sides, axis=1), leaf_panel[c], NT)

    def coupling(group, _):
        ps = [group * (width // 2) + i for i in range(width // 2)]
        pairs = [(one_leaf(2 * p), one_leaf(2 * p + 1)) for p in ps]
        for p, pair in zip(ps, pairs):
            leaf_sum[p] = jnp.concatenate(pair, axis=1)
        return 0

    per_piece = parents // (pieces // 2)
    for piece in range(pieces // 2):
        lax.fori_loop(piece * per_piece * 2 // width, (piece + 1) * per_piece * 2 // width, coupling, 0)
        advance(pieces // 2 + piece)

    for h in range(1 << nbits):
        for z in range(line):
            for part in range(parts):
                arrived((h * 2 + 1 - core) * line + z, part)
    loads[4].wait()

    low_half = lax.broadcasted_iota(jnp.int32, (half, 2 * rank), 1) < rank

    def remote_rows(p):
        tiles = [gathered[owner[k, p] * parents + local[k, p]] for k in range(kp)]
        upper, lower = [], []
        for k in range(0, kp, 2):
            a, b = tiles[k], tiles[k + 1]
            turned_a = jnp.concatenate([a[:, rank:], a[:, :rank]], axis=1)
            turned_b = jnp.concatenate([b[:, rank:], b[:, :rank]], axis=1)
            upper.append(jnp.where(low_half, a, turned_b))
            lower.append(jnp.where(low_half, turned_a, b))
        return jnp.concatenate(
            [jnp.concatenate(upper, axis=1), jnp.concatenate(lower, axis=1)], axis=0)

    def downward(group, _):
        ps = [group * width + i for i in range(width)]
        fields = [dot(remote_rows(p), parent_panel[p], NT).astype(jnp.bfloat16) for p in ps]
        totals = [leaf_sum[p] + dot(field, transfer[p], NN) for p, field in zip(ps, fields)]
        fars = []
        for p, total in zip(ps, totals):
            zero = jnp.zeros_like(total)
            stacked = jnp.concatenate(
                [jnp.where(low_lanes, total, zero), jnp.where(low_lanes, zero, total)], axis=0)
            weights = basis[pl.ds(2 * p, 2)].reshape(2 * rank, size)
            fars.append(dot(stacked.astype(jnp.bfloat16), weights, NN))
        for p, far in zip(ps, fars):
            out[2 * p] = (far[:rhs] + near_sum[2 * p]).astype(jnp.bfloat16)
            out[2 * p + 1] = (far[rhs:] + near_sum[2 * p + 1]).astype(jnp.bfloat16)
        return 0

    stores = []
    per_part = groups // out_parts
    for part in range(out_parts):
        lax.fori_loop(part * per_part, (part + 1) * per_part, downward, 0)
        rows = pl.ds(2 * part * per_part * width, 2 * per_part * width)
        stores.append(pltpu.make_async_copy(out.at[rows], out_hbm.at[rows], out_sem.at[part]))
        stores[-1].start()
    for copy in sends:
        copy.wait_send()
    for copy in stores:
        copy.wait()


def on_device(
    streams,
    line,
    points_rhs,
    leaf_basis,
    transfer,
    leaf_coupling,
    parent_coupling,
    near_blocks,
    near_offsets,
    coupling_offsets,
    parent_owner,
    parent_local,
):
    leaves, rhs, size = points_rhs.shape
    parents, rank, _ = transfer.shape
    places = streams // 2
    nbits = bits_of(places)
    blocks = streams * line
    copies = (line - 1) + line * (places - 1) + line * places
    smem = pl.BlockSpec(memory_space=pltpu.SMEM)
    hbm = pl.BlockSpec(memory_space=pl.ANY)
    bf16 = jnp.bfloat16
    dma = pltpu.SemaphoreType.DMA
    near_parts, out_parts = 4, 4
    parts = 2
    return pl.pallas_call(
        functools.partial(kernel, streams, line),
        out_shape=jax.ShapeDtypeStruct(points_rhs.shape, bf16),
        in_specs=[smem] * 4 + [hbm] * 6,
        out_specs=hbm,
        scratch_shapes=[
            pltpu.VMEM((leaves + 2 * NEAR_REACH, rhs, size), bf16),
            pltpu.VMEM(leaf_basis.shape, bf16),
            pltpu.VMEM(transfer.shape, bf16),
            pltpu.VMEM(leaf_coupling.shape, bf16),
            pltpu.VMEM(parent_coupling.shape, bf16),
            pltpu.VMEM(near_blocks.shape, bf16),
            pltpu.VMEM((leaves + 2 * FAR_REACH, rhs, 2 * rank), bf16),
            pltpu.VMEM((blocks * parents, rhs // 2, 2 * rank), bf16),
            pltpu.VMEM((leaves, rhs, size), jnp.float32),
            pltpu.VMEM((parents, rhs, 2 * rank), jnp.float32),
            pltpu.VMEM((leaves, rhs, size), bf16),
            dma((5,)),
            dma((near_parts,)),
            dma((out_parts,)),
            dma((4,)),
            dma((4,)),
            dma((copies * parts,)),
            dma((blocks * parts,)),
        ],
        compiler_params=pltpu.CompilerParams(collective_id=0, has_side_effects=True),
    )(
        near_offsets.T, coupling_offsets.T, parent_owner.T, parent_local.T,
        points_rhs, leaf_basis, transfer, leaf_coupling, parent_coupling, near_blocks,
    )


def solution(mesh):
    whole = P(("stream", "leaf"))
    return jax.shard_map(
        functools.partial(on_device, mesh.shape["stream"], mesh.shape["leaf"]),
        mesh=mesh,
        in_specs=(whole,) * 10,
        out_specs=whole,
        check_vma=False,
    )
```

profile of v0, /device:TPU:9, one launch (start us, length us, event | category | flops | bytes accessed | tf_op | source)
XLA Modules:
  0.0 39.5 jit_solution(18166368389727520475)
XLA Ops:
  0.0 37.7 %shard_map.100 = bf16[64,32,128]{2,1,0:T(8,128)(2,1)} custom-call(s32[3,64]{1,0:T(4,128)} %bitcast.6, s32[4,64]{1,0:T(4,128)} %bitcast.7, s32[8,32]{1,0:T(8,128)} %bitcast.4, s32[8,32]{1,0:T(8,128)} %bitcast.5, bf16[64,32,128]{2,1,0:T(8,128)(2,1)} %points_hbm.1, bf16[64,64,128]{2,1,0:T(8,128)(2,1)} %basis_hbm.1, bf16[32,64,128]{2,1,0:T(8,128)(2,1)} %transfer_hbm.1, ...), custom_call_target="tpu_custom_call" | custom-call | tf_op jit(solution)/shard_map/pallas_call | solution.py:366
  37.7 1.9 %copy.12 = bf16[64,32,128]{2,1,0:T(8,128)(2,1)} copy(bf16[64,32,128]{2,1,0:T(8,128)(2,1)} %shard_map.100) | data formatting | bytes 1048576
where the time goes:
time: 39.7 us; the launch traced here: 39.5 us
  Pallas kernels  37.7 us (95%)
  local copies, waits for them, and re-layouts  1.87 us (5%)
    pallas_call x1, Pallas kernels, on_device(): pl.pallas_call(functools.partial(kernel, streams, line), out_shape=jax.Sh...  37.7 us
    unnamed x1, local copies, waits for them, and re-layouts  1.87 us

commit v1 on v0

v1 whole, which is shorter than its diff:
```python
import functools

import jax
import jax.numpy as jnp
from jax import lax
from jax.experimental import pallas as pl
from jax.experimental.pallas import tpu as pltpu
from jax.sharding import PartitionSpec as P

NEAR_REACH = 2
FAR_REACH = 5
MESH = pl.DeviceIdType.MESH
NT = (((1,), (1,)), ((), ()))
NN = (((1,), (0,)), ((), ()))


WIDTH = 8
PARTS = 4
CLOCK, NEAR_TIME, FAR_TIME = 1.0, 0.8, 0.4
READY_TIME, EDGE_TIME = 7.0, 12.0
WINDOWS = {
    (0, 1): (2.3, 4.8),
    (1, 0): (2.3, 4.8),
    (2, 0): (2.3, 4.8),
    (0, 2): (3.5, 6.0),
    (3, 0): (5.0, 7.5),
    (0, 3): (6.0, 9.0),
    (1, 2): (7.5, 10.5),
    (2, 2): (7.5, 10.5),
    (1, 1): (10.0, 14.0),
    (2, 1): (13.0, 16.0),
    (1, 3): (10.0, 13.5),
    (2, 3): (10.0, 13.5),
    (3, 2): (10.0, 13.0),
    (3, 1): (13.0, 17.0),
    (3, 3): (13.0, 17.0),
}
LATE = {1: (8.5, 10.5), 2: (10.5, 12.5)}


def line_order(line):
    table = [sorted(range(line), key=lambda other: ((other // 2 != z // 2) + (other != z), abs(other - z), other))
             for z in range(line)]
    for z in range(line):
        for other in range(line):
            if abs(other - z) > 1:
                nearer = z + (1 if other > z else -1)
                assert table[nearer].index(other) <= table[z].index(other)
    return table


def sends_of(line, nbits):
    sends = nbits + 3
    for step in range(line):
        for mask in range(1 << nbits):
            if mask or step:
                sends += 1 + (mask == 0)
                sends += 2 * bool(mask and mask & (mask - 1) == 0 and step == 0)
                sends += 0 if mask == 0 and step == 1 else nbits - mask.bit_length()
    return sends


def dot(a, b, dims):
    return lax.dot_general(a, b, dims, preferred_element_type=jnp.float32)


def bits_of(count):
    bits = count.bit_length() - 1
    assert 1 << bits == count
    return bits


def kernel(
    streams, line, parts,
    near_off_hbm, far_off_hbm, owner_hbm, local_hbm,
    points_hbm, basis_hbm, transfer_hbm, leaf_hbm, parent_hbm, near_hbm,
    out_hbm,
    near_off, far_off, owner, local,
    points, points_low, points_high, basis, transfer, leaf_panel, parent_panel, near_blocks,
    coeffs, coeffs_low, coeffs_high, gathered, near_sum, leaf_sum, out,
    index_sem, load_sem, edge_sem, near_sem, panel_sem, out_sem,
    halo_send, halo_recv, send_sem, recv_sem, ready,
):
    leaves, rhs, size = points_hbm.shape
    parents, rank, _ = transfer_hbm.shape
    kn = near_off.shape[0]
    kc = far_off.shape[0]
    kp = owner.shape[0]
    half = rhs // 2
    width = WIDTH
    groups = parents // width
    near_edge = points_low.shape[0] - NEAR_REACH
    far_edge = coeffs_low.shape[0] - FAR_REACH
    chunk = parents // parts
    nbits = bits_of(streams // 2)
    bits_of(line)
    assert line > 1
    near_parts = near_sem.shape[0]
    out_parts = out_sem.shape[0]

    my_s = lax.axis_index("stream")
    my_z = lax.axis_index("leaf")
    core = my_s % 2
    place = my_s // 2
    total_blocks = streams * line
    me = my_s * line + my_z

    def device(block):
        return (block // line, block % line)

    def block_of(h, z):
        return (h * 2 + core) * line + z

    def bit_at(phase):
        first = 1 << phase
        if nbits < 2:
            return first
        second = 1 << ((phase + 1) % nbits)
        return first + core * (second - first)

    def flip(h, bit):
        return h + bit * (1 - 2 * ((h // bit) % 2))

    def subset(mask):
        h = place
        for phase in range(nbits):
            if mask >> phase & 1:
                h = flip(h, bit_at(phase))
        return h

    table = line_order(line)
    planes = [my_z]
    for step in range(1, line):
        z = table[0][step]
        for row in range(1, line):
            z = jnp.where(my_z == row, table[row][step], z)
        planes.append(z)
    pair_z = flip(my_z, 1)
    cross_z = 2 * my_z - pair_z
    crosses = (cross_z >= 0) & (cross_z < line)
    cross_z = jnp.clip(cross_z, 0, line - 1)

    partners = [(flip(place, bit_at(i)) * 2 + core, my_z) for i in range(nbits)]
    pair = (my_s, pair_z)
    cross = (my_s, cross_z)
    sibling = (my_s + 1 - 2 * core, my_z)
    after = device((me + 1) % total_blocks)
    before = device((me + total_blocks - 1) % total_blocks)
    starts_line = my_z == 0
    ends_line = my_z == line - 1

    indices = [
        pltpu.make_async_copy(source, target, index_sem.at[i])
        for i, (source, target) in enumerate([
            (near_off_hbm, near_off), (far_off_hbm, far_off),
            (owner_hbm, owner), (local_hbm, local)])
    ]
    loads = [
        [pltpu.make_async_copy(source.at[pl.ds(g * step, step)],
                               target.at[pl.ds(g * step, step)], load_sem.at[3 * g + i])
         for i, (source, target, step) in enumerate([
             (points_hbm, points, 2 * width), (basis_hbm, basis, 2 * width),
             (transfer_hbm, transfer, width)])]
        for g in range(groups)
    ]
    edges = [
        pltpu.make_async_copy(points_hbm.at[pl.ds(0, near_edge)],
                              points_low.at[pl.ds(NEAR_REACH, near_edge)], edge_sem.at[0]),
        pltpu.make_async_copy(points_hbm.at[pl.ds(leaves - near_edge, near_edge)],
                              points_high.at[pl.ds(0, near_edge)], edge_sem.at[1]),
    ]
    panels = [
        pltpu.make_async_copy(leaf_hbm, leaf_panel, panel_sem.at[0]),
        pltpu.make_async_copy(parent_hbm, parent_panel, panel_sem.at[1]),
    ]
    near_rows = leaves // near_parts
    near_loads = [
        pltpu.make_async_copy(
            near_hbm.at[pl.ds(i * near_rows, near_rows)],
            near_blocks.at[pl.ds(i * near_rows, near_rows)],
            near_sem.at[i],
        )
        for i in range(near_parts)
    ]
    barrier = pltpu.get_barrier_semaphore()
    for load in loads[0]:
        load.start()
    greeted = partners + [pair, sibling]
    for other in greeted:
        pl.semaphore_signal(barrier, inc=1, device_id=other, device_id_type=MESH)

    @pl.when(crosses)
    def _():
        pl.semaphore_signal(barrier, inc=1, device_id=cross, device_id_type=MESH)

    @pl.when(starts_line)
    def _():
        pl.semaphore_signal(barrier, inc=1, device_id=before, device_id_type=MESH)

    for group in loads[1:]:
        for load in group:
            load.start()
    for load in indices + edges + near_loads + panels:
        load.start()

    low_lanes = lax.broadcasted_iota(jnp.int32, (rhs, 2 * rank), 1) < rank

    def upward(group):
        ps = [group * width + i for i in range(width)]
        boths = []
        for p in ps:
            pair = jnp.concatenate([points[2 * p], points[2 * p + 1]], axis=0)
            weights = basis[pl.ds(2 * p, 2)].reshape(2 * rank, size)
            boths.append(dot(pair, weights, NT))
        sides = [jnp.where(low_lanes, both[:rhs], both[rhs:]) for both in boths]
        ups = [dot(side.astype(jnp.bfloat16), transfer[p], NT) for p, side in zip(ps, sides)]
        for p, up in zip(ps, ups):
            packed = jnp.concatenate([up[:half], up[half:]], axis=1)
            gathered[me * parents + p] = packed.astype(jnp.bfloat16)
        for p, side in zip(ps, sides):
            rolled = pltpu.roll(side, rank, 1)
            for c, value in ((2 * p, jnp.where(low_lanes, side, rolled).astype(jnp.bfloat16)),
                             (2 * p + 1, jnp.where(low_lanes, rolled, side).astype(jnp.bfloat16))):
                coeffs[c] = value
                if c < far_edge:
                    coeffs_low[FAR_REACH + c] = value
                if c >= leaves - far_edge:
                    coeffs_high[c - (leaves - far_edge)] = value

    def halo(index, source, target, whom):
        return pltpu.make_async_remote_copy(
            src_ref=source, dst_ref=target,
            send_sem=halo_send.at[index], recv_sem=halo_recv.at[index],
            device_id=whom, device_id_type=MESH,
        )

    point_halos = [
        halo(0, points.at[pl.ds(leaves - NEAR_REACH, NEAR_REACH)],
             points_low.at[pl.ds(0, NEAR_REACH)], after),
        halo(1, points.at[pl.ds(0, NEAR_REACH)],
             points_high.at[pl.ds(near_edge, NEAR_REACH)], before),
    ]
    coeff_halos = [
        halo(2, coeffs.at[pl.ds(leaves - FAR_REACH, FAR_REACH)],
             coeffs_low.at[pl.ds(0, FAR_REACH)], after),
        halo(3, coeffs.at[pl.ds(0, FAR_REACH)],
             coeffs_high.at[pl.ds(far_edge, FAR_REACH)], before),
    ]

    sends = []

    def when(condition, action):
        if condition is None:
            action()
        else:
            pl.when(condition)(action)

    def span(block, part):
        return gathered.at[pl.ds(block * parents + part * chunk, chunk)]

    def send(block, part, whom, condition=None):
        copy = pltpu.make_async_remote_copy(
            src_ref=span(block, part), dst_ref=span(block, part),
            send_sem=send_sem.at[len(sends)], recv_sem=recv_sem.at[block * parts + part],
            device_id=whom, device_id_type=MESH,
        )
        when(condition, copy.start)
        sends.append((condition, copy))

    def arrived(block, part):
        pltpu.make_async_remote_copy(
            src_ref=span(block, part), dst_ref=span(block, part),
            send_sem=send_sem.at[0], recv_sem=recv_sem.at[block * parts + part],
            device_id=sibling, device_id_type=MESH,
        ).wait_recv()

    per_part = groups // parts
    for part in range(parts):
        for group in range(part * per_part, (part + 1) * per_part):
            for load in loads[group]:
                load.wait()
            upward(group)
        if part == 0:
            pl.semaphore_wait(barrier, len(greeted) + crosses.astype(jnp.int32) + ends_line.astype(jnp.int32))

            @pl.when(ends_line)
            def _():
                pl.semaphore_signal(ready, inc=1, device_id=after, device_id_type=MESH)

        send(me, part, pair)
        send(me, part, cross, crosses)
        for whom in partners + [sibling]:
            send(me, part, whom)

    for copy in (point_halos[0], coeff_halos[0]):
        copy.start()

    def send_back():
        for copy in (point_halos[1], coeff_halos[1]):
            copy.start()

    @pl.when(jnp.logical_not(starts_line))
    def _():
        send_back()

    def single(mask):
        return mask and mask & (mask - 1) == 0

    def relay(mask, step, part):
        block = block_of(subset(mask), planes[step])
        arrived(block, part)
        if mask == 0:
            onward = 2 * (planes[step] < my_z).astype(jnp.int32) - 1
            z = my_z + onward
            send(block, part, (my_s, jnp.clip(z, 0, line - 1)), (z >= 0) & (z < line))
        if single(mask) and step == 0:
            send(block, part, pair, jnp.logical_not(crosses))
        if not (mask == 0 and step == 1):
            for phase in range(mask.bit_length(), nbits):
                send(block, part, partners[phase])
        send(block, part, sibling)

    def relay_late(mask, step, part):
        send(block_of(subset(mask), planes[step]), part, pair, crosses)

    def window(mask, step):
        bits = bin(mask).count("1")
        if nbits == 2 and line == 4:
            return WINDOWS[(mask, step)]
        begin = 4 * bits + 3 * step
        return (begin, begin + 3.0)

    events = []
    for step in range(line):
        for mask in range(1 << nbits):
            if mask or step:
                spans = [(relay, window(mask, step))]
                if single(mask) and step == 0:
                    late = 6 if mask.bit_length() < nbits else 9
                    spans.append((relay_late, LATE[mask] if nbits == 2 and line == 4 else (late, late + 3.0)))
                for action, (begin, end) in spans:
                    for part in range(parts):
                        time = begin + (end - begin) * (part + 1) / parts
                        events.append((time, len(events), functools.partial(action, mask, step, part)))

    def send_back_late():
        @pl.when(starts_line)
        def _():
            pl.semaphore_wait(ready, 1)
            send_back()

    events.append((READY_TIME, len(events), send_back_late))
    events.sort()

    clock = [CLOCK]

    def advance(time):
        clock[0] += time
        while events and events[0][0] <= clock[0]:
            events.pop(0)[2]()

    first = me == 0
    last = me == total_blocks - 1

    def near(group, rows_of, shift):
        cs = [group * width + i for i in range(width)]
        sums = []
        for c in cs:
            rows = [rows_of[c + shift + near_off[k, c]] for k in range(kn)]
            weights = [near_blocks[c, k] for k in range(kn)]
            sums.append(dot(jnp.concatenate(rows, axis=1), jnp.concatenate(weights, axis=1), NT))
        for c, value in zip(cs, sums):
            near_sum[c] = value

    def one_leaf(c, rows_of, shift):
        rows = [rows_of[c + shift + far_off[k, c]] for k in range(kc)]
        sides = [jnp.where(low_lanes, rows[k], rows[k + 1]) for k in range(0, kc, 2)]
        return dot(jnp.concatenate(sides, axis=1), leaf_panel[c], NT)

    def coupling(group, rows_of, shift):
        ps = [group * (width // 2) + i for i in range(width // 2)]
        pairs = [(one_leaf(2 * p, rows_of, shift), one_leaf(2 * p + 1, rows_of, shift)) for p in ps]
        for p, pair in zip(ps, pairs):
            leaf_sum[p] = jnp.concatenate(pair, axis=1)

    leaf_groups = leaves // width
    inner = list(range(1, leaf_groups - 1))
    for copy in indices:
        copy.wait()
    loaded = set()

    def near_piece(group, rows_of, shift):
        part = group * width // near_rows
        if part not in loaded:
            near_loads[part].wait()
            loaded.add(part)
        near(group, rows_of, shift)
        advance(NEAR_TIME)

    for group in inner:
        near_piece(group, points, 0)
    panels[0].wait()
    for group in inner:
        coupling(group, coeffs, 0)
        advance(FAR_TIME)

    advance(EDGE_TIME - clock[0])
    for copy in edges + point_halos + coeff_halos:
        copy.wait()

    @pl.when(first)
    def _():
        points_low[pl.ds(0, NEAR_REACH)] = jnp.zeros((NEAR_REACH, rhs, size), jnp.bfloat16)
        coeffs_low[pl.ds(0, FAR_REACH)] = jnp.zeros((FAR_REACH, rhs, 2 * rank), jnp.bfloat16)

    @pl.when(last)
    def _():
        points_high[pl.ds(near_edge, NEAR_REACH)] = jnp.zeros((NEAR_REACH, rhs, size), jnp.bfloat16)
        coeffs_high[pl.ds(far_edge, FAR_REACH)] = jnp.zeros((FAR_REACH, rhs, 2 * rank), jnp.bfloat16)

    near_piece(0, points_low, NEAR_REACH)
    near_piece(leaf_groups - 1, points_high, near_edge - leaves)
    coupling(0, coeffs_low, FAR_REACH)
    advance(FAR_TIME)
    coupling(leaf_groups - 1, coeffs_high, far_edge - leaves)
    advance(1e9)

    for h in range(1 << nbits):
        for z in range(line):
            for part in range(parts):
                arrived((h * 2 + 1 - core) * line + z, part)
    panels[1].wait()

    low_half = lax.broadcasted_iota(jnp.int32, (half, 2 * rank), 1) < rank

    def remote_rows(p):
        tiles = [gathered[owner[k, p] * parents + local[k, p]] for k in range(kp)]
        upper, lower = [], []
        for k in range(0, kp, 2):
            a, b = tiles[k], tiles[k + 1]
            turned_a = jnp.concatenate([a[:, rank:], a[:, :rank]], axis=1)
            turned_b = jnp.concatenate([b[:, rank:], b[:, :rank]], axis=1)
            upper.append(jnp.where(low_half, a, turned_b))
            lower.append(jnp.where(low_half, turned_a, b))
        return jnp.concatenate(
            [jnp.concatenate(upper, axis=1), jnp.concatenate(lower, axis=1)], axis=0)

    def downward(group, _):
        ps = [group * width + i for i in range(width)]
        fields = [dot(remote_rows(p), parent_panel[p], NT).astype(jnp.bfloat16) for p in ps]
        totals = [leaf_sum[p] + dot(field, transfer[p], NN) for p, field in zip(ps, fields)]
        fars = []
        for p, total in zip(ps, totals):
            zero = jnp.zeros_like(total)
            stacked = jnp.concatenate(
                [jnp.where(low_lanes, total, zero), jnp.where(low_lanes, zero, total)], axis=0)
            weights = basis[pl.ds(2 * p, 2)].reshape(2 * rank, size)
            fars.append(dot(stacked.astype(jnp.bfloat16), weights, NN))
        for p, far in zip(ps, fars):
            out[2 * p] = (far[:rhs] + near_sum[2 * p]).astype(jnp.bfloat16)
            out[2 * p + 1] = (far[rhs:] + near_sum[2 * p + 1]).astype(jnp.bfloat16)
        return 0

    stores = []
    per_part = groups // out_parts
    for part in range(out_parts):
        lax.fori_loop(part * per_part, (part + 1) * per_part, downward, 0)
        rows = pl.ds(2 * part * per_part * width, 2 * per_part * width)
        stores.append(pltpu.make_async_copy(out.at[rows], out_hbm.at[rows], out_sem.at[part]))
        stores[-1].start()
    for condition, copy in sends:
        when(condition, copy.wait_send)
    for copy in stores:
        copy.wait()


def on_device(
    streams,
    line,
    points_rhs,
    leaf_basis,
    transfer,
    leaf_coupling,
    parent_coupling,
    near_blocks,
    near_offsets,
    coupling_offsets,
    parent_owner,
    parent_local,
):
    leaves, rhs, size = points_rhs.shape
    parents, rank, _ = transfer.shape
    places = streams // 2
    nbits = bits_of(places)
    blocks = streams * line
    parts, near_parts, out_parts = PARTS, 4, 4
    copies = sends_of(line, nbits) * parts
    hbm = pl.BlockSpec(memory_space=pl.ANY)
    bf16 = jnp.bfloat16
    dma = pltpu.SemaphoreType.DMA
    near_edge, far_edge = WIDTH + NEAR_REACH, WIDTH + FAR_REACH
    groups = parents // WIDTH
    offsets = [x.T for x in (near_offsets, coupling_offsets, parent_owner, parent_local)]
    return pl.pallas_call(
        functools.partial(kernel, streams, line, parts),
        out_shape=jax.ShapeDtypeStruct(points_rhs.shape, bf16),
        in_specs=[hbm] * 10,
        out_specs=hbm,
        scratch_shapes=[
            *[pltpu.SMEM(x.shape, jnp.int32) for x in offsets],
            pltpu.VMEM(points_rhs.shape, bf16),
            pltpu.VMEM((near_edge + NEAR_REACH, rhs, size), bf16),
            pltpu.VMEM((near_edge + NEAR_REACH, rhs, size), bf16),
            pltpu.VMEM(leaf_basis.shape, bf16),
            pltpu.VMEM(transfer.shape, bf16),
            pltpu.VMEM(leaf_coupling.shape, bf16),
            pltpu.VMEM(parent_coupling.shape, bf16),
            pltpu.VMEM(near_blocks.shape, bf16),
            pltpu.VMEM((leaves, rhs, 2 * rank), bf16),
            pltpu.VMEM((far_edge + FAR_REACH, rhs, 2 * rank), bf16),
            pltpu.VMEM((far_edge + FAR_REACH, rhs, 2 * rank), bf16),
            pltpu.VMEM((blocks * parents, rhs // 2, 2 * rank), bf16),
            pltpu.VMEM((leaves, rhs, size), jnp.float32),
            pltpu.VMEM((parents, rhs, 2 * rank), jnp.float32),
            pltpu.VMEM((leaves, rhs, size), bf16),
            dma((4,)),
            dma((3 * groups,)),
            dma((2,)),
            dma((near_parts,)),
            dma((2,)),
            dma((out_parts,)),
            dma((4,)),
            dma((4,)),
            dma((copies,)),
            dma((blocks * parts,)),
            pltpu.SemaphoreType.REGULAR,
        ],
        compiler_params=pltpu.CompilerParams(collective_id=0, has_side_effects=True),
    )(
        *offsets,
        points_rhs, leaf_basis, transfer, leaf_coupling, parent_coupling, near_blocks,
    )


def solution(mesh):
    whole = P(("stream", "leaf"))
    return jax.shard_map(
        functools.partial(on_device, mesh.shape["stream"], mesh.shape["leaf"]),
        mesh=mesh,
        in_specs=(whole,) * 10,
        out_specs=whole,
        check_vma=False,
    )
```

time: 39.7 us -> 34.1 us (0.86)
  the two profiles are of different devices: /device:TPU:9 before, /device:TPU:1 now
where the time goes in v1:
time: 34.1 us; the launch traced here: 33.9 us
  Pallas kernels  32 us (94%)
  local copies, waits for them, and re-layouts  1.87 us (5%)
    pallas_call x1, Pallas kernels, on_device(): pl.pallas_call(functools.partial(kernel, streams, line, parts), out_shape...  32 us
    unnamed x1, local copies, waits for them, and re-layouts  1.87 us

profile of v1, /device:TPU:1, one launch (start us, length us, event | category | flops | bytes accessed | tf_op | source)
XLA Modules:
  0.0 33.9 jit_solution(16617784374520587412)
XLA Ops:
  0.0 32.0 %shard_map.100 = bf16[64,32,128]{2,1,0:T(8,128)(2,1)} custom-call(s32[3,64]{1,0:T(4,128)} %bitcast.6, s32[4,64]{1,0:T(4,128)} %bitcast.7, s32[8,32]{1,0:T(8,128)} %bitcast.4, s32[8,32]{1,0:T(8,128)} %bitcast.5, bf16[64,32,128]{2,1,0:T(8,128)(2,1)} %points_hbm.1, bf16[64,64,128]{2,1,0:T(8,128)(2,1)} %basis_hbm.1, bf16[32,64,128]{2,1,0:T(8,128)(2,1)} %transfer_hbm.1, ...), custom_call_target="tpu_custom_call" | custom-call | tf_op jit(solution)/shard_map/pallas_call | solution.py:504
  32.0 1.9 %copy.12 = bf16[64,32,128]{2,1,0:T(8,128)(2,1)} copy(bf16[64,32,128]{2,1,0:T(8,128)(2,1)} %shard_map.100) | data formatting | bytes 1048576

commit v2 on v1

--- a/solution.py
+++ b/solution.py
@@ -15,27 +15,45 @@
 
 
 WIDTH = 8
+VMEM_LIMIT = 40 << 20
 PARTS = 4
 CLOCK, NEAR_TIME, FAR_TIME = 1.0, 0.8, 0.4
-READY_TIME, EDGE_TIME = 7.0, 12.0
-WINDOWS = {
+READY_TIME, EDGE_TIME = 4.4, 14.2
+MIDDLE = {
+    (0, 1): (1.2, 4.0),
+    (1, 0): (2.3, 4.8),
+    (2, 0): (2.3, 4.8),
+    (0, 2): (0.6, 2.8),
+    (0, 3): (4.0, 8.0),
+    (1, 2): (5.0, 9.0),
+    (2, 2): (9.5, 11.0),
+    (1, 1): (11.0, 13.0),
+    (1, 3): (11.0, 13.0),
+    (2, 1): (13.0, 14.0),
+    (2, 3): (12.5, 14.0),
+    (3, 0): (13.9, 14.1),
+    (3, 2): (14.4, 15.0),
+    (3, 1): (15.0, 17.0),
+    (3, 3): (15.5, 17.5),
+}
+END = {
     (0, 1): (2.3, 4.8),
     (1, 0): (2.3, 4.8),
     (2, 0): (2.3, 4.8),
     (0, 2): (3.5, 6.0),
-    (3, 0): (5.0, 7.5),
     (0, 3): (6.0, 9.0),
-    (1, 2): (7.5, 10.5),
-    (2, 2): (7.5, 10.5),
-    (1, 1): (10.0, 14.0),
-    (2, 1): (13.0, 16.0),
-    (1, 3): (10.0, 13.5),
-    (2, 3): (10.0, 13.5),
-    (3, 2): (10.0, 13.0),
-    (3, 1): (13.0, 17.0),
-    (3, 3): (13.0, 17.0),
+    (1, 2): (9.5, 11.0),
+    (2, 2): (9.5, 11.0),
+    (1, 1): (11.0, 13.0),
+    (1, 3): (11.0, 13.0),
+    (2, 1): (13.0, 14.0),
+    (2, 3): (12.5, 14.0),
+    (3, 0): (13.9, 14.1),
+    (3, 2): (14.4, 15.0),
+    (3, 1): (15.0, 17.0),
+    (3, 3): (15.5, 17.5),
 }
-LATE = {1: (8.5, 10.5), 2: (10.5, 12.5)}
+LATE = {1: (8.2, 8.6), 2: (9.0, 10.0)}
 
 
 def line_order(line):
@@ -74,11 +92,11 @@
     streams, line, parts,
     near_off_hbm, far_off_hbm, owner_hbm, local_hbm,
     points_hbm, basis_hbm, transfer_hbm, leaf_hbm, parent_hbm, near_hbm,
-    out_hbm,
+    out,
     near_off, far_off, owner, local,
     points, points_low, points_high, basis, transfer, leaf_panel, parent_panel, near_blocks,
-    coeffs, coeffs_low, coeffs_high, gathered, near_sum, leaf_sum, out,
-    index_sem, load_sem, edge_sem, near_sem, panel_sem, out_sem,
+    coeffs, coeffs_low, coeffs_high, gathered, near_sum, leaf_sum,
+    index_sem, load_sem, edge_sem, near_sem, panel_sem,
     halo_send, halo_recv, send_sem, recv_sem, ready,
 ):
     leaves, rhs, size = points_hbm.shape
@@ -96,7 +114,6 @@
     bits_of(line)
     assert line > 1
     near_parts = near_sem.shape[0]
-    out_parts = out_sem.shape[0]
 
     my_s = lax.axis_index("stream")
     my_z = lax.axis_index("leaf")
@@ -247,7 +264,7 @@
              coeffs_high.at[pl.ds(far_edge, FAR_REACH)], before),
     ]
 
-    sends = []
+    sends = {}
 
     def when(condition, action):
         if condition is None:
@@ -258,14 +275,19 @@
     def span(block, part):
         return gathered.at[pl.ds(block * parents + part * chunk, chunk)]
 
-    def send(block, part, whom, condition=None):
-        copy = pltpu.make_async_remote_copy(
+    def send(name, block, part, whom, condition=None):
+        index, _ = sends.setdefault((name, part), (len(sends), condition))
+        when(condition, pltpu.make_async_remote_copy(
             src_ref=span(block, part), dst_ref=span(block, part),
-            send_sem=send_sem.at[len(sends)], recv_sem=recv_sem.at[block * parts + part],
+            send_sem=send_sem.at[index], recv_sem=recv_sem.at[block * parts + part],
             device_id=whom, device_id_type=MESH,
-        )
-        when(condition, copy.start)
-        sends.append((condition, copy))
+        ).start)
+
+    def sent(index):
+        pltpu.make_async_remote_copy(
+            src_ref=span(me, 0), dst_ref=span(me, 0), send_sem=send_sem.at[index], recv_sem=recv_sem.at[0],
+            device_id=sibling, device_id_type=MESH,
+        ).wait_send()
 
     def arrived(block, part):
         pltpu.make_async_remote_copy(
@@ -287,10 +309,11 @@
             def _():
                 pl.semaphore_signal(ready, inc=1, device_id=after, device_id_type=MESH)
 
-        send(me, part, pair)
-        send(me, part, cross, crosses)
-        for whom in partners + [sibling]:
-            send(me, part, whom)
+        send("own pair", me, part, pair)
+        send("own cross", me, part, cross, crosses)
+        for phase, whom in enumerate(partners):
+            send(("own", phase), me, part, whom)
+        send("own sibling", me, part, sibling)
 
     for copy in (point_halos[0], coeff_halos[0]):
         copy.start()
@@ -305,43 +328,53 @@
 
     def single(mask):
         return mask and mask & (mask - 1) == 0
+
+    onward = []
+    for step in range(line):
+        up = planes[step] < my_z
+        z = jnp.where(up, my_z + 1, my_z - 1)
+        needed = (z >= 0) & (z < line)
+        onward.append(((my_s, jnp.clip(z, 0, line - 1)), needed))
 
     def relay(mask, step, part):
         block = block_of(subset(mask), planes[step])
         arrived(block, part)
         if mask == 0:
-            onward = 2 * (planes[step] < my_z).astype(jnp.int32) - 1
-            z = my_z + onward
-            send(block, part, (my_s, jnp.clip(z, 0, line - 1)), (z >= 0) & (z < line))
+            whom, needed = onward[step]
+            send((mask, step, "onward"), block, part, whom, needed)
         if single(mask) and step == 0:
-            send(block, part, pair, jnp.logical_not(crosses))
+            send((mask, step, "pair"), block, part, pair, jnp.logical_not(crosses))
         if not (mask == 0 and step == 1):
             for phase in range(mask.bit_length(), nbits):
-                send(block, part, partners[phase])
-        send(block, part, sibling)
+                send((mask, step, phase), block, part, partners[phase])
+        send((mask, step, "sibling"), block, part, sibling)
 
     def relay_late(mask, step, part):
-        send(block_of(subset(mask), planes[step]), part, pair, crosses)
-
-    def window(mask, step):
-        bits = bin(mask).count("1")
+        send((mask, step, "late"), block_of(subset(mask), planes[step]), part, pair, crosses)
+
+    def windows(mask, step):
         if nbits == 2 and line == 4:
-            return WINDOWS[(mask, step)]
-        begin = 4 * bits + 3 * step
-        return (begin, begin + 3.0)
+            return MIDDLE[(mask, step)], END[(mask, step)]
+        begin = 4 * bin(mask).count("1") + 3 * step
+        return ((begin, begin + 3.0),) * 2
 
     events = []
     for step in range(line):
         for mask in range(1 << nbits):
             if mask or step:
-                spans = [(relay, window(mask, step))]
-                if single(mask) and step == 0:
-                    late = 6 if mask.bit_length() < nbits else 9
-                    spans.append((relay_late, LATE[mask] if nbits == 2 and line == 4 else (late, late + 3.0)))
-                for action, (begin, end) in spans:
-                    for part in range(parts):
-                        time = begin + (end - begin) * (part + 1) / parts
-                        events.append((time, len(events), functools.partial(action, mask, step, part)))
+                for part in range(parts):
+                    action = functools.partial(relay, mask, step, part)
+                    middle, end = [begin + (till - begin) * (part + 1) / parts for begin, till in windows(mask, step)]
+                    if middle == end:
+                        events.append((end, len(events), action))
+                    else:
+                        events.append((middle, len(events), functools.partial(when, crosses, action)))
+                        events.append((end, len(events), functools.partial(when, jnp.logical_not(crosses), action)))
+                    if single(mask) and step == 0:
+                        begin = 6.0 if mask.bit_length() < nbits else 9.0
+                        begin, till = LATE[mask] if nbits == 2 and line == 4 else (begin, begin + 3.0)
+                        time = begin + (till - begin) * (part + 1) / parts
+                        events.append((time, len(events), functools.partial(relay_late, mask, step, part)))
 
     def send_back_late():
         @pl.when(starts_line)
@@ -461,17 +494,10 @@
             out[2 * p + 1] = (far[rhs:] + near_sum[2 * p + 1]).astype(jnp.bfloat16)
         return 0
 
-    stores = []
-    per_part = groups // out_parts
-    for part in range(out_parts):
-        lax.fori_loop(part * per_part, (part + 1) * per_part, downward, 0)
-        rows = pl.ds(2 * part * per_part * width, 2 * per_part * width)
-        stores.append(pltpu.make_async_copy(out.at[rows], out_hbm.at[rows], out_sem.at[part]))
-        stores[-1].start()
-    for condition, copy in sends:
-        when(condition, copy.wait_send)
-    for copy in stores:
-        copy.wait()
+    for part in range(groups):
+        downward(part, 0)
+    for index, condition in sends.values():
+        when(condition, functools.partial(sent, index))
 
 
 def on_device(
@@ -493,9 +519,9 @@
     places = streams // 2
     nbits = bits_of(places)
     blocks = streams * line
-    parts, near_parts, out_parts = PARTS, 4, 4
+    parts, near_parts = PARTS, 4
     copies = sends_of(line, nbits) * parts
-    hbm = pl.BlockSpec(memory_space=pl.ANY)
+    hbm = pl.BlockSpec(memory_space=pltpu.HBM)
     bf16 = jnp.bfloat16
     dma = pltpu.SemaphoreType.DMA
     near_edge, far_edge = WIDTH + NEAR_REACH, WIDTH + FAR_REACH
@@ -505,7 +531,7 @@
         functools.partial(kernel, streams, line, parts),
         out_shape=jax.ShapeDtypeStruct(points_rhs.shape, bf16),
         in_specs=[hbm] * 10,
-        out_specs=hbm,
+        out_specs=pl.BlockSpec(memory_space=pltpu.VMEM),
         scratch_shapes=[
             *[pltpu.SMEM(x.shape, jnp.int32) for x in offsets],
             pltpu.VMEM(points_rhs.shape, bf16),
@@ -522,23 +548,22 @@
             pltpu.VMEM((blocks * parents, rhs // 2, 2 * rank), bf16),
             pltpu.VMEM((leaves, rhs, size), jnp.float32),
             pltpu.VMEM((parents, rhs, 2 * rank), jnp.float32),
-            pltpu.VMEM((leaves, rhs, size), bf16),
             dma((4,)),
             dma((3 * groups,)),
             dma((2,)),
             dma((near_parts,)),
             dma((2,)),
-            dma((out_parts,)),
             dma((4,)),
             dma((4,)),
             dma((copies,)),
             dma((blocks * parts,)),
             pltpu.SemaphoreType.REGULAR,
         ],
-        compiler_params=pltpu.CompilerParams(collective_id=0, has_side_effects=True),
+        compiler_params=pltpu.CompilerParams(
+            collective_id=0, has_side_effects=True, vmem_limit_bytes=VMEM_LIMIT),
     )(
-        *offsets,
-        points_rhs, leaf_basis, transfer, leaf_coupling, parent_coupling, near_blocks,
+        *[pltpu.with_memory_space_constraint(x, pltpu.HBM) for x in (
+            *offsets, points_rhs, leaf_basis, transfer, leaf_coupling, parent_coupling, near_blocks)]
     )
 
 

time: 34.1 us -> 31.7 us (0.930)
  Pallas kernels: 32 us -> 30.8 us
  local copies, waits for them, and re-layouts: 1.87 us -> 0.8 us
    pallas_call x1, Pallas kernels: 32 us -> 30.8 us  [on_device(): pl.pallas_call(functools.partial(kernel, streams, line, parts), out_shape...]
    unnamed x1, local copies, waits for them, and re-layouts: 1.87 us -> 0.8 us
where the time goes in v2:
time: 31.7 us; the launch traced here: 31.6 us
  Pallas kernels  30.8 us (97%)
  local copies, waits for them, and re-layouts  0.8 us (3%)
    pallas_call x1, Pallas kernels, on_device(): pl.pallas_call(functools.partial(kernel, streams, line, parts), out_shape...  30.8 us
    unnamed x1, local copies, waits for them, and re-layouts  0.8 us

profile of v2, /device:TPU:1, one launch (start us, length us, event | category | flops | bytes accessed | tf_op | source)
XLA Modules:
  0.0 31.6 jit_solution(4294083298646042508)
XLA Ops:
  0.0 30.8 %shard_map.100 = bf16[64,32,128]{2,1,0:T(8,128)(2,1)S(1)} custom-call(s32[3,64]{1,0:T(4,128)} %bitcast.6, s32[4,64]{1,0:T(4,128)} %bitcast.7, s32[8,32]{1,0:T(8,128)} %bitcast.4, s32[8,32]{1,0:T(8,128)} %bitcast.5, bf16[64,32,128]{2,1,0:T(8,128)(2,1)} %points_hbm.1, bf16[64,64,128]{2,1,0:T(8,128)(2,1)} %basis_hbm.1, bf16[32,64,128]{2,1,0:T(8,128)(2,1)} %transfer_hbm.1, ...), custom_call_target="tpu_custom_call" | custom-call | tf_op jit(solution)/shard_map/pallas_call | solution.py:530
  30.8 0.8 %copy.12 = bf16[64,32,128]{2,1,0:T(8,128)(2,1)} copy(bf16[64,32,128]{2,1,0:T(8,128)(2,1)S(1)} %shard_map.100) | data formatting | bytes 1048576

commit v3 on v2

--- a/solution.py
+++ b/solution.py
@@ -97,7 +97,7 @@
     points, points_low, points_high, basis, transfer, leaf_panel, parent_panel, near_blocks,
     coeffs, coeffs_low, coeffs_high, gathered, near_sum, leaf_sum,
     index_sem, load_sem, edge_sem, near_sem, panel_sem,
-    halo_send, halo_recv, send_sem, recv_sem, ready,
+    halo_send, halo_recv, send_sem, recv_sem, sibling_sem, ready,
 ):
     leaves, rhs, size = points_hbm.shape
     parents, rank, _ = transfer_hbm.shape
@@ -155,6 +155,7 @@
     pair_z = flip(my_z, 1)
     cross_z = 2 * my_z - pair_z
     crosses = (cross_z >= 0) & (cross_z < line)
+    ends = (cross_z < 0) | (cross_z >= line)
     cross_z = jnp.clip(cross_z, 0, line - 1)
 
     partners = [(flip(place, bit_at(i)) * 2 + core, my_z) for i in range(nbits)]
@@ -275,26 +276,30 @@
     def span(block, part):
         return gathered.at[pl.ds(block * parents + part * chunk, chunk)]
 
-    def send(name, block, part, whom, condition=None):
-        index, _ = sends.setdefault((name, part), (len(sends), condition))
+    tallies = {}
+
+    def send(name, block, part, whom, condition=None, group="all"):
+        if group == "all":
+            group = (group, len([1 for other in sends.values() if other[0] == "all"]) // (total_blocks * parts))
+        group = sends.setdefault((name, part), group)
+        index, _ = tallies.setdefault(group, (len(tallies), condition))
+        arrives = sibling_sem.at[0] if whom is sibling else recv_sem.at[slot(block, part)]
         when(condition, pltpu.make_async_remote_copy(
             src_ref=span(block, part), dst_ref=span(block, part),
-            send_sem=send_sem.at[index], recv_sem=recv_sem.at[block * parts + part],
+            send_sem=send_sem.at[index], recv_sem=arrives,
             device_id=whom, device_id_type=MESH,
         ).start)
 
-    def sent(index):
-        pltpu.make_async_remote_copy(
-            src_ref=span(me, 0), dst_ref=span(me, 0), send_sem=send_sem.at[index], recv_sem=recv_sem.at[0],
-            device_id=sibling, device_id_type=MESH,
-        ).wait_send()
+    def slot(block, part):
+        return (block // (2 * line) * line + block % line) * parts + part
+
+    def moved(rows, sent, received):
+        return pltpu.make_async_remote_copy(
+            src_ref=gathered.at[pl.ds(0, rows)], dst_ref=gathered.at[pl.ds(0, rows)],
+            send_sem=sent, recv_sem=received, device_id=sibling, device_id_type=MESH)
 
     def arrived(block, part):
-        pltpu.make_async_remote_copy(
-            src_ref=span(block, part), dst_ref=span(block, part),
-            send_sem=send_sem.at[0], recv_sem=recv_sem.at[block * parts + part],
-            device_id=sibling, device_id_type=MESH,
-        ).wait_recv()
+        moved(chunk, send_sem.at[0], recv_sem.at[slot(block, part)]).wait_recv()
 
     per_part = groups // parts
     for part in range(parts):
@@ -310,7 +315,7 @@
                 pl.semaphore_signal(ready, inc=1, device_id=after, device_id_type=MESH)
 
         send("own pair", me, part, pair)
-        send("own cross", me, part, cross, crosses)
+        send("own cross", me, part, cross, crosses, "crosses")
         for phase, whom in enumerate(partners):
             send(("own", phase), me, part, whom)
         send("own sibling", me, part, sibling)
@@ -341,16 +346,16 @@
         arrived(block, part)
         if mask == 0:
             whom, needed = onward[step]
-            send((mask, step, "onward"), block, part, whom, needed)
+            send((mask, step, "onward"), block, part, whom, needed, ("onward", step))
         if single(mask) and step == 0:
-            send((mask, step, "pair"), block, part, pair, jnp.logical_not(crosses))
+            send((mask, step, "pair"), block, part, pair, ends, "ends")
         if not (mask == 0 and step == 1):
             for phase in range(mask.bit_length(), nbits):
                 send((mask, step, phase), block, part, partners[phase])
         send((mask, step, "sibling"), block, part, sibling)
 
     def relay_late(mask, step, part):
-        send((mask, step, "late"), block_of(subset(mask), planes[step]), part, pair, crosses)
+        send((mask, step, "late"), block_of(subset(mask), planes[step]), part, pair, crosses, "crosses")
 
     def windows(mask, step):
         if nbits == 2 and line == 4:
@@ -458,10 +463,7 @@
     coupling(leaf_groups - 1, coeffs_high, far_edge - leaves)
     advance(1e9)
 
-    for h in range(1 << nbits):
-        for z in range(line):
-            for part in range(parts):
-                arrived((h * 2 + 1 - core) * line + z, part)
+    moved(total_blocks // 2 * parents, send_sem.at[0], sibling_sem.at[0]).wait_recv()
     panels[1].wait()
 
     low_half = lax.broadcasted_iota(jnp.int32, (half, 2 * rank), 1) < rank
@@ -496,8 +498,9 @@
 
     for part in range(groups):
         downward(part, 0)
-    for index, condition in sends.values():
-        when(condition, functools.partial(sent, index))
+    for group, (index, condition) in tallies.items():
+        rows = chunk * list(sends.values()).count(group)
+        when(condition, moved(rows, send_sem.at[index], sibling_sem.at[0]).wait_send)
 
 
 def on_device(
@@ -520,7 +523,6 @@
     nbits = bits_of(places)
     blocks = streams * line
     parts, near_parts = PARTS, 4
-    copies = sends_of(line, nbits) * parts
     hbm = pl.BlockSpec(memory_space=pltpu.HBM)
     bf16 = jnp.bfloat16
     dma = pltpu.SemaphoreType.DMA
@@ -555,8 +557,9 @@
             dma((2,)),
             dma((4,)),
             dma((4,)),
-            dma((copies,)),
-            dma((blocks * parts,)),
+            dma((line + 3 + sends_of(line, nbits) // blocks,)),
+            dma((blocks // 2 * parts,)),
+            dma((1,)),
             pltpu.SemaphoreType.REGULAR,
         ],
         compiler_params=pltpu.CompilerParams(

time: 31.7 us -> 29.8 us (0.940)
  Pallas kernels: 30.8 us -> 28.9 us
    pallas_call x1, Pallas kernels: 30.8 us -> 28.9 us  [on_device(): pl.pallas_call(functools.partial(kernel, streams, line, parts), out_shape...]
where the time goes in v3:
time: 29.8 us; the launch traced here: 29.7 us
  Pallas kernels  28.9 us (97%)
  local copies, waits for them, and re-layouts  0.8 us (3%)
    pallas_call x1, Pallas kernels, on_device(): pl.pallas_call(functools.partial(kernel, streams, line, parts), out_shape...  28.9 us
    unnamed x1, local copies, waits for them, and re-layouts  0.8 us

profile of v3, /device:TPU:1, one launch (start us, length us, event | category | flops | bytes accessed | tf_op | source)
XLA Modules:
  0.0 29.7 jit_solution(18229737198593413792)
XLA Ops:
  0.0 28.9 %shard_map.100 = bf16[64,32,128]{2,1,0:T(8,128)(2,1)S(1)} custom-call(s32[3,64]{1,0:T(4,128)} %bitcast.6, s32[4,64]{1,0:T(4,128)} %bitcast.7, s32[8,32]{1,0:T(8,128)} %bitcast.4, s32[8,32]{1,0:T(8,128)} %bitcast.5, bf16[64,32,128]{2,1,0:T(8,128)(2,1)} %points_hbm.1, bf16[64,64,128]{2,1,0:T(8,128)(2,1)} %basis_hbm.1, bf16[32,64,128]{2,1,0:T(8,128)(2,1)} %transfer_hbm.1, ...), custom_call_target="tpu_custom_call" | custom-call | tf_op jit(solution)/shard_map/pallas_call | solution.py:532
  28.9 0.8 %copy.12 = bf16[64,32,128]{2,1,0:T(8,128)(2,1)} copy(bf16[64,32,128]{2,1,0:T(8,128)(2,1)S(1)} %shard_map.100) | data formatting | bytes 1048576

commit v4 on v3

--- a/solution.py
+++ b/solution.py
@@ -15,6 +15,7 @@
 
 
 WIDTH = 8
+DOWN_WIDTH = 32
 VMEM_LIMIT = 40 << 20
 PARTS = 4
 CLOCK, NEAR_TIME, FAR_TIME = 1.0, 0.8, 0.4
@@ -26,8 +27,8 @@
     (0, 2): (0.6, 2.8),
     (0, 3): (4.0, 8.0),
     (1, 2): (5.0, 9.0),
-    (2, 2): (9.5, 11.0),
-    (1, 1): (11.0, 13.0),
+    (2, 2): (12.0, 13.0),
+    (1, 1): (11.5, 13.0),
     (1, 3): (11.0, 13.0),
     (2, 1): (13.0, 14.0),
     (2, 3): (12.5, 14.0),
@@ -43,8 +44,8 @@
     (0, 2): (3.5, 6.0),
     (0, 3): (6.0, 9.0),
     (1, 2): (9.5, 11.0),
-    (2, 2): (9.5, 11.0),
-    (1, 1): (11.0, 13.0),
+    (2, 2): (12.0, 13.0),
+    (1, 1): (11.5, 13.0),
     (1, 3): (11.0, 13.0),
     (2, 1): (13.0, 14.0),
     (2, 3): (12.5, 14.0),
@@ -480,8 +481,8 @@
         return jnp.concatenate(
             [jnp.concatenate(upper, axis=1), jnp.concatenate(lower, axis=1)], axis=0)
 
-    def downward(group, _):
-        ps = [group * width + i for i in range(width)]
+    def downward(group):
+        ps = [group * DOWN_WIDTH + i for i in range(DOWN_WIDTH)]
         fields = [dot(remote_rows(p), parent_panel[p], NT).astype(jnp.bfloat16) for p in ps]
         totals = [leaf_sum[p] + dot(field, transfer[p], NN) for p, field in zip(ps, fields)]
         fars = []
@@ -494,10 +495,9 @@
         for p, far in zip(ps, fars):
             out[2 * p] = (far[:rhs] + near_sum[2 * p]).astype(jnp.bfloat16)
             out[2 * p + 1] = (far[rhs:] + near_sum[2 * p + 1]).astype(jnp.bfloat16)
-        return 0
-
-    for part in range(groups):
-        downward(part, 0)
+
+    for group in range(parents // DOWN_WIDTH):
+        downward(group)
     for group, (index, condition) in tallies.items():
         rows = chunk * list(sends.values()).count(group)
         when(condition, moved(rows, send_sem.at[index], sibling_sem.at[0]).wait_send)

time: 29.8 us -> 29.3 us (0.983)
  Pallas kernels: 28.9 us -> 28.3 us
    pallas_call x1, Pallas kernels: 28.9 us -> 28.3 us  [on_device(): pl.pallas_call(functools.partial(kernel, streams, line, parts), out_shape...]
where the time goes in v4:
time: 29.3 us; the launch traced here: 29.2 us
  Pallas kernels  28.3 us (97%)
  local copies, waits for them, and re-layouts  0.8 us (3%)
    pallas_call x1, Pallas kernels, on_device(): pl.pallas_call(functools.partial(kernel, streams, line, parts), out_shape...  28.3 us
    unnamed x1, local copies, waits for them, and re-layouts  0.8 us

profile of v4, /device:TPU:1, one launch (start us, length us, event | category | flops | bytes accessed | tf_op | source)
XLA Modules:
  0.0 29.2 jit_solution(15009654371153931695)
XLA Ops:
  0.0 28.3 %shard_map.100 = bf16[64,32,128]{2,1,0:T(8,128)(2,1)S(1)} custom-call(s32[3,64]{1,0:T(4,128)} %bitcast.6, s32[4,64]{1,0:T(4,128)} %bitcast.7, s32[8,32]{1,0:T(8,128)} %bitcast.4, s32[8,32]{1,0:T(8,128)} %bitcast.5, bf16[64,32,128]{2,1,0:T(8,128)(2,1)} %points_hbm.1, bf16[64,64,128]{2,1,0:T(8,128)(2,1)} %basis_hbm.1, bf16[32,64,128]{2,1,0:T(8,128)(2,1)} %transfer_hbm.1, ...), custom_call_target="tpu_custom_call" | custom-call | tf_op jit(solution)/shard_map/pallas_call | solution.py:532
  28.4 0.8 %copy.12 = bf16[64,32,128]{2,1,0:T(8,128)(2,1)} copy(bf16[64,32,128]{2,1,0:T(8,128)(2,1)S(1)} %shard_map.100) | data formatting | bytes 1048576
